TPU v7x, 32 devices: a whole 2x2x4 slice. The times are simulated.
32 devices in a mesh: member: 8 (over y, x, core), dp: 4 (over z).
Axes of the slice: x: 2, y: 2, z: 4, core: 2. Of those that a mesh axis runs over, the one named last changes fastest.
Arguments:
- trunk: bfloat16 [1576, 1024], P('dp'), may hold values from -6 to 6
- normgain: float32 [1024], replicated, may hold values from 0.25 to 1.75
- expand: bfloat16 [1024, 2048], P('member'), may hold values from -0.1875 to 0.1875
- shrink: bfloat16 [2048, 1024], P('member'), may hold values from -0.125 to 0.125
- inscale: float32 [8, 1024], P('member'), may hold values from 0.25 to 1.75
- hidscale: float32 [8, 2048], P('member'), may hold values from 0.25 to 1.75
- actscale: float32 [8, 2048], P('member'), may hold values from 0.25 to 1.75
- outscale: float32 [8, 1024], P('member'), may hold values from 0.25 to 1.75
- cotangent: bfloat16 [8, 1576, 1024], P('member', 'dp'), may hold values from -6 to 6
Outputs:
- trunk_grad: bfloat16 [1576, 1024], P('dp', 'member')
- expand_grad: float32 [1024, 2048], P('member')
- shrink_grad: float32 [2048, 1024], P('member')
- inscale_grad: float32 [8, 1024], P('member')
- hidscale_grad: float32 [8, 2048], P('member')
- actscale_grad: float32 [8, 2048], P('member')
- outscale_grad: float32 [8, 1024], P('member')
- normgain_grad: float32 [1024], replicated
All inputs are finite; a program needn't handle non-finite values.
Results may differ from a plain program's by a relative error of at most 0.024.
Values may be sent and summed in bfloat16 or wider, within the bound.
A program may use at most 64 MiB of HBM per device.

v0:
```python
import functools

import jax
import jax.numpy as jnp
from jax import lax
from jax.experimental import pallas as pl
from jax.experimental.pallas import tpu as pltpu
from jax.sharding import PartitionSpec as P

eps = 1e-06
coeff = 0.7978845608028654
MESH = pl.DeviceIdType.MESH
F32, BF16 = jnp.float32, jnp.bfloat16


def gelu_pair(hidden):
    inner = coeff * (hidden + 0.044715 * hidden * hidden * hidden)
    tangent = jnp.tanh(inner)
    active = 0.5 * hidden * (1.0 + tangent)
    slope = 0.5 * (1.0 + tangent) + 0.5 * hidden * (1.0 - tangent * tangent) * coeff * (
        1.0 + 3.0 * 0.044715 * hidden * hidden
    )
    return (active, slope)


def dot(a, b, da, db):
    return lax.dot_general(a, b, (((da,), (db,)), ((), ())), preferred_element_type=F32)


def kernel(
    n, nz,
    trunk, gain, expand, shrink, r_in, r_out, r_hid, r_act, cot,
    o_trunk, o_expand, o_shrink, o_small,
    scales, e_all, et, sc_all, cots, si_all, proj_all, act_all, slope_all, sa_all, normed_ref, inv_ref,
    b_acc, s_acc, e_acc, g_acc,
    e_send, e_recv, s_send, t_sum, u_send, u_recv, t_send, t_recv,
    s_in1, s_part, s_in2, s_fin, e_in1, e_part, e_in2, e_fin, t_in1, t_part, t_in2, t_fin,
    sem_es, sem_er, sem_ss, sem_sr, sem_cs, sem_cr, sem_fs, sem_ps,
    sem_gs, sem_gr, sem_us, sem_ur, sem_ts, sem_tr,
    sem_zs, sem_ze, sem_zt,
):
    me = lax.axis_index("member")
    mz = lax.axis_index("dp")
    tok, d = trunk.shape
    ff = expand.shape[1]
    fs = ff // n
    ds = d // n
    half = d // 2
    gy = 2
    gx = n // (2 * gy)
    core, xx, yy = me % 2, (me // 2) % gx, me // (2 * gx)

    def peer(s):
        c = (core + s % 2) % 2
        a = (xx + (s // 2) % gx) % gx
        b = (yy + s // (2 * gx)) % gy
        return (b * gx + a) * 2 + c

    def zpeer(k):
        return (mz + k) % nz

    def remote(src, dst, ss, rs, axis, who):
        return pltpu.make_async_remote_copy(
            src_ref=src, dst_ref=dst, send_sem=ss, recv_sem=rs,
            device_id={axis: who}, device_id_type=MESH,
        )

    scales[:, pl.ds(0, d)] = r_in[...]
    scales[:, pl.ds(d, d)] = r_out[...]
    scales[:, pl.ds(2 * d, ff)] = r_hid[...]
    scales[:, pl.ds(2 * d + ff, ff)] = r_act[...]

    barrier = pltpu.get_barrier_semaphore()
    for s in range(1, n):
        pl.semaphore_signal(barrier, inc=1, device_id={"member": peer(s)}, device_id_type=MESH)
    for k in range(1, nz):
        pl.semaphore_signal(barrier, inc=1, device_id={"dp": zpeer(k)}, device_id_type=MESH)
    pl.semaphore_wait(barrier, n - 1 + nz - 1)

    def e_cp(s):
        p = peer(s)
        return remote(
            expand.at[:, pl.ds(pl.multiple_of(p * fs, fs), fs)], e_all.at[me],
            sem_es.at[s], sem_er.at[me], "member", p)

    def sc_cp(s):
        return remote(scales, sc_all.at[me], sem_ss.at[s], sem_sr.at[me], "member", peer(s))

    def hs(h):
        return pl.ds(h * half, half)

    def own_cp(s, h):
        return remote(
            cot.at[:, hs(h)], cots.at[me, :, hs(h)], sem_cs.at[s, h], sem_cr.at[me, h],
            "member", peer(s))

    def fwd_cp(m, h, s, sem):
        return remote(
            cots.at[m, :, hs(h)], cots.at[m, :, hs(h)], sem, sem_cr.at[m, h], "member", peer(s))

    def cot_wait(m, h):
        fwd_cp(m, h, 1, sem_fs.at[0]).wait_recv()

    order = [s for s in range(2, n)] + [1]
    for s in order:
        sc_cp(s).start()
        e_cp(s).start()
    square = n == 8
    own_sends = [(1, 0), (1, 1)]
    if square:
        own_sends += [(2, 0), (4, 1), (2, 1), (4, 0)]
    else:
        own_sends += [(s, h) for s in range(2, n, 2) for h in range(2)]
    for s, h in own_sends:
        own_cp(s, h).start()

    e_all[me] = expand[:, pl.ds(pl.multiple_of(me * fs, fs), fs)]
    sc_all[me] = scales[...]
    cots[me] = cot[...]

    tokens = trunk[...].astype(F32)
    centered = tokens - jnp.mean(tokens, axis=1, keepdims=True)
    inv = lax.rsqrt(jnp.mean(centered * centered, axis=1, keepdims=True) + eps)
    normed_ref[...] = centered * inv
    inv_ref[...] = inv
    b_acc[...] = jnp.zeros_like(b_acc)
    s_acc[...] = jnp.zeros_like(s_acc)
    e_acc[...] = jnp.zeros_like(e_acc)
    g_acc[...] = jnp.zeros_like(g_acc)

    for s in order:
        p = peer(s)
        remote(scales, sc_all.at[p], sem_ss.at[s], sem_sr.at[p], "member", p).wait_recv()
        remote(e_all.at[p], e_all.at[p], sem_es.at[s], sem_er.at[p], "member", p).wait_recv()

    et[...] = e_all[...].reshape(d, fs).T

    def scale_rows(m):
        a = sc_all[m, :, pl.ds(0, d)]
        b = sc_all[m, :, pl.ds(d, d)]
        c = sc_all[m, :, pl.ds(pl.multiple_of(2 * d + me * fs, fs), fs)]
        e = sc_all[m, :, pl.ds(pl.multiple_of(2 * d + ff + me * fs, fs), fs)]
        return a, b, c, e

    @pl.loop(0, n)
    def _(s):
        m = peer(s)
        s_in, s_out, s_hid, s_act = scale_rows(m)
        si = (normed_ref[...] * gain[...] * s_in).astype(BF16)
        si_all[s] = si
        proj = dot(si, e_all[...].reshape(d, fs), 1, 0)
        active, slope = gelu_pair(proj * s_hid)
        proj_all[s] = proj
        act_all[s] = active
        slope_all[s] = slope * s_act
        sa_all[s] = (active * s_act).astype(BF16)

    @pl.loop(0, n)
    def _(s):
        m = peer(s)
        if square:
            @pl.when(s == 1)
            def _():
                cot_wait(peer(2), 0)
                fwd_cp(peer(2), 0, 4, sem_fs.at[0]).start()
                cot_wait(peer(4), 1)
                fwd_cp(peer(4), 1, 2, sem_fs.at[1]).start()

            @pl.when((s % 2 == 1) | (s == 6))
            def _():
                cot_wait(m, 0)
                cot_wait(m, 1)

            @pl.when(s == 2)
            def _():
                cot_wait(m, 1)

            @pl.when(s == 4)
            def _():
                cot_wait(m, 0)
        else:
            @pl.when(s > 0)
            def _():
                cot_wait(m, 0)
                cot_wait(m, 1)

        @pl.when((s % 2 == 0) & (s > 0))
        def _():
            for h in range(2):
                fwd_cp(m, h, 1, sem_ps.at[s, h]).start()

        s_in, s_out, s_hid, s_act = scale_rows(m)
        upstream = cots[m].astype(F32)
        scaled_cot = (upstream * s_out).astype(BF16)
        back_act = dot(scaled_cot, shrink[...], 1, 1)
        g_act = jnp.sum(back_act * act_all[s], axis=0, keepdims=True)
        back_hid = back_act * slope_all[s]
        g_hid = jnp.sum(back_hid * proj_all[s], axis=0, keepdims=True)
        back_proj = (back_hid * s_hid).astype(BF16)
        s_term = dot(sa_all[s], scaled_cot, 0, 0)
        s_acc[...] += s_term
        g_out = jnp.sum(s_term * shrink[...].astype(F32), axis=0, keepdims=True) / s_out
        e_term = dot(back_proj, si_all[s], 0, 0)
        e_acc[...] += e_term
        e_sum = jnp.sum(e_term * et[...].astype(F32), axis=0, keepdims=True)
        g_acc[...] += e_sum
        b_acc[...] += dot(back_proj, et[...], 1, 0) * s_in
        t_send[m, :, pl.ds(0, d)] = e_sum / s_in
        t_send[m, :, pl.ds(d, d)] = g_out
        t_send[m, :, pl.ds(3 * d, fs)] = g_hid
        t_send[m, :, pl.ds(3 * d + fs, fs)] = g_act

    chain = nz == 4
    inner = (mz == 1) | (mz == 2)
    outer = (mz == 0) | (mz == 3)
    pair = mz + 1 - 2 * (mz % 2)
    across = 3 - mz

    class Reduce:
        def __init__(self, own, in1, part, in2, fin, sem):
            self.refs, self.sem = (own, in1, part, in2, fin), sem

        def hop(self, k, q):
            own, in1, part, in2, fin = self.refs
            src, dst, who = ((own, in1, pair), (part, in2, across), (fin, fin, pair))[k]
            return remote(src.at[q], dst.at[q], self.sem.at[2 * k, q], self.sem.at[2 * k + 1, q], "dp", who)

        def start(self, q):
            if chain:
                @pl.when(outer)
                def _():
                    self.hop(0, q).start()

        def mid(self, q):
            own, in1, part, in2, fin = self.refs
            if chain:
                @pl.when(inner)
                def _():
                    self.hop(0, q).wait_recv()
                    part[q] = (own[q].astype(F32) + in1[q].astype(F32)).astype(part.dtype)
                    self.hop(1, q).start()

        def fin(self, q):
            own, in1, part, in2, fin = self.refs
            if chain:
                @pl.when(inner)
                def _():
                    self.hop(1, q).wait_recv()
                    fin[q] = (part[q].astype(F32) + in2[q].astype(F32)).astype(fin.dtype)
                    self.hop(2, q).start()

        def end(self, q):
            if chain:
                @pl.when(outer)
                def _():
                    self.hop(2, q).wait_recv()

        def sent(self, q):
            if chain:
                @pl.when(outer)
                def _():
                    self.hop(0, q).wait_send()

                @pl.when(inner)
                def _():
                    self.hop(1, q).wait_send()
                    self.hop(2, q).wait_send()

        def whole(self, k, slot):
            own, in1 = self.refs[:2]
            return remote(own, in1.at[slot], self.sem.at[0, k], self.sem.at[1, slot], "dp", zpeer(k))

        def plain(self):
            own, in1, part, in2, fin = self.refs
            for k in range(1, nz):
                self.whole(k, mz).start()
            in1[mz] = own[...]
            for k in range(1, nz):
                self.whole(k, zpeer(k)).wait_recv()
            fin[...] = sum(in1[z].astype(F32) for z in range(nz)).astype(fin.dtype)
            for k in range(1, nz):
                self.whole(k, mz).wait_send()

    red_s = Reduce(s_send, s_in1, s_part, s_in2, s_fin, sem_zs)
    red_e = Reduce(e_recv, e_in1, e_part, e_in2, e_fin, sem_ze)
    red_t = Reduce(t_sum, t_in1, t_part, t_in2, t_fin, sem_zt)

    rz = s_acc.shape[0] // nz
    for q in range(nz):
        s_send[q] = s_acc[pl.ds(q * rz, rz), :].astype(BF16)
        red_s.start(q)

    ez = ds // nz
    e_t = e_acc[...].T.astype(BF16)
    for p in range(n):
        for q in range(nz):
            e_send[p, q] = e_t[p * ds + q * ez:p * ds + (q + 1) * ez, :]
    for s in order:
        p = peer(s)
        remote(e_send.at[p], e_recv.at[:, me], sem_gs.at[s], sem_gr.at[me], "member", p).start()
    e_recv[:, me] = e_send[me]

    g_part = g_acc[...] / gain[...]
    for p in range(n):
        t_send[p, :, pl.ds(2 * d, d)] = g_part
    for s in order:
        p = peer(s)
        remote(t_send.at[p], t_recv.at[me], sem_ts.at[s], sem_tr.at[me], "member", p).start()
    t_recv[me] = t_send[me]

    unit = b_acc[...] * gain[...]
    normed = normed_ref[...]
    term = cot[...].astype(F32) + inv_ref[...] * (
        unit
        - jnp.mean(unit, axis=1, keepdims=True)
        - normed * jnp.mean(unit * normed, axis=1, keepdims=True)
    )
    term = term.astype(BF16)
    for p in range(n):
        u_send[p] = term[:, p * ds:(p + 1) * ds]
    for s in order:
        p = peer(s)
        remote(u_send.at[p], u_recv.at[me], sem_us.at[s], sem_ur.at[me], "member", p).start()

    red_s.mid(0)
    red_s.mid(1)
    if chain:
        red_s.mid(2)
        red_s.fin(0)

    for s in order:
        p = peer(s)
        remote(t_send.at[p], t_recv.at[p], sem_ts.at[s], sem_tr.at[p], "member", p).wait_recv()
    t_sum[0, :, pl.ds(0, 3 * d)] = sum(t_recv[p, :, pl.ds(0, 3 * d)] for p in range(n))
    for p in range(n):
        t_sum[0, :, pl.ds(3 * d + p * fs, fs)] = t_recv[p, :, pl.ds(3 * d, fs)]
        t_sum[0, :, pl.ds(3 * d + ff + p * fs, fs)] = t_recv[p, :, pl.ds(3 * d + fs, fs)]
    red_t.start(0)

    for s in order:
        p = peer(s)
        remote(e_send.at[p], e_recv.at[:, p], sem_gs.at[s], sem_gr.at[p], "member", p).wait_recv()
    if chain:
        for q in range(nz):
            red_e.start(q)
        red_s.mid(3)
        red_s.fin(1)
        red_t.mid(0)
        red_s.fin(2)
        red_s.fin(3)
        red_e.mid(0)
        red_t.fin(0)
        red_e.mid(1)
    else:
        red_s.plain()
        red_t.plain()
        red_e.plain()

    total = u_send[me].astype(F32)
    for s in order:
        p = peer(s)
        remote(u_send.at[p], u_recv.at[p], sem_us.at[s], sem_ur.at[p], "member", p).wait_recv()
        total += u_recv[p].astype(F32)
    o_trunk[...] = total.astype(BF16)

    if chain:
        red_e.mid(2)
        red_e.fin(0)
        red_e.mid(3)
        red_e.fin(1)
        red_e.fin(2)
        red_e.fin(3)
        for q in range(nz):
            red_s.end(q)
        red_t.end(0)
    o_shrink[...] = s_fin[...]
    o_small[...] = t_fin[0]
    if chain:
        for q in range(nz):
            red_e.end(q)
            o_expand[q] = e_fin[q]
            red_s.sent(q)
            red_e.sent(q)
        red_t.sent(0)
    else:
        o_expand[...] = e_fin[...]

    for s in order:
        p = peer(s)
        sc_cp(s).wait_send()
        e_cp(s).wait_send()
        remote(e_send.at[p], e_recv.at[:, me], sem_gs.at[s], sem_gr.at[me], "member", p).wait_send()
        remote(t_send.at[p], t_recv.at[me], sem_ts.at[s], sem_tr.at[me], "member", p).wait_send()
        remote(u_send.at[p], u_recv.at[me], sem_us.at[s], sem_ur.at[me], "member", p).wait_send()
    for s, h in own_sends:
        own_cp(s, h).wait_send()
    if square:
        fwd_cp(peer(2), 0, 4, sem_fs.at[0]).wait_send()
        fwd_cp(peer(4), 1, 2, sem_fs.at[1]).wait_send()
    for s in range(2, n, 2):
        for h in range(2):
            fwd_cp(peer(s), h, 1, sem_ps.at[s, h]).wait_send()


def finish(n, nz, trunk, expand, shrink, small, o_trunk, o_expand, o_shrink, o_in, o_hid, o_act, o_out, o_gain):
    d, ff = o_in.shape[1], o_hid.shape[1]
    ez, rz, fs = expand.shape[2], shrink.shape[1], expand.shape[3]
    o_trunk[...] = trunk[...]
    o_in[...] = small[:, pl.ds(0, d)]
    o_out[...] = small[:, pl.ds(d, d)]
    o_gain[...] = small[:, pl.ds(2 * d, d)]
    o_hid[...] = small[:, pl.ds(3 * d, ff)]
    o_act[...] = small[:, pl.ds(3 * d + ff, ff)]
    for q in range(nz):
        o_shrink[pl.ds(q * rz, rz), :] = shrink[q].astype(F32)
        for p in range(n):
            o_expand[pl.ds(q * ez, ez), pl.ds(p * fs, fs)] = expand[q, p].astype(F32)


def body(n, nz, trunk, normgain, expand, shrink, inscale, hidscale, actscale, outscale, cotangent):
    tok, d = trunk.shape
    ff = expand.shape[1]
    fs, ds = ff // n, d // n
    rz, ez = fs // nz, ds // nz
    width = 2 * d + 2 * ff
    V = pltpu.VMEM
    DMA = pltpu.SemaphoreType.DMA
    small, small2 = 3 * d + 2 * fs, 3 * d + 2 * ff

    def buffers(shape, dtype):
        first = shape if nz == 4 else (nz, *shape)
        return V(first, dtype), V(shape, dtype), V(shape, dtype), V(shape, dtype)

    parts = pl.pallas_call(
        functools.partial(kernel, n, nz),
        out_shape=[
            jax.ShapeDtypeStruct((tok, ds), BF16),
            jax.ShapeDtypeStruct((nz, n, ez, fs), BF16),
            jax.ShapeDtypeStruct((nz, rz, d), BF16),
            jax.ShapeDtypeStruct((1, small2), F32),
        ],
        in_specs=[pl.BlockSpec(memory_space=V)] * 9,
        out_specs=[pl.BlockSpec(memory_space=V)] * 4,
        scratch_shapes=[
            V((1, width), F32), V((n, ds, fs), BF16), V((fs, d), BF16), V((n, 1, width), F32),
            V((n, tok, d), BF16), V((n, tok, d), BF16),
            V((n, tok, fs), F32), V((n, tok, fs), F32), V((n, tok, fs), F32), V((n, tok, fs), BF16),
            V((tok, d), F32), V((tok, 1), F32),
            V((tok, d), F32), V((fs, d), F32), V((fs, d), F32), V((1, d), F32),
            V((n, nz, ez, fs), BF16), V((nz, n, ez, fs), BF16), V((nz, rz, d), BF16), V((1, 1, small2), F32),
            V((n, tok, ds), BF16), V((n, tok, ds), BF16),
            V((n, 1, small), F32), V((n, 1, small), F32),
            *buffers((nz, rz, d), BF16), *buffers((nz, n, ez, fs), BF16), *buffers((1, 1, small2), F32),
            DMA((n,)), DMA((n,)), DMA((n,)), DMA((n,)), DMA((n, 2)), DMA((n, 2)), DMA((2,)), DMA((n, 2)),
            DMA((n,)), DMA((n,)), DMA((n,)), DMA((n,)), DMA((n,)), DMA((n,)),
            DMA((6, nz)), DMA((6, nz)), DMA((6, nz)),
        ],
        compiler_params=pltpu.CompilerParams(
            collective_id=0, has_side_effects=True, vmem_limit_bytes=64000 * 1024
        ),
    )(trunk, normgain[None], expand, shrink, inscale, outscale, hidscale, actscale, cotangent[0])
    out = pl.pallas_call(
        functools.partial(finish, n, nz),
        out_shape=[
            jax.ShapeDtypeStruct((tok, ds), BF16),
            jax.ShapeDtypeStruct((ds, ff), F32),
            jax.ShapeDtypeStruct((fs, d), F32),
            jax.ShapeDtypeStruct((1, d), F32),
            jax.ShapeDtypeStruct((1, ff), F32),
            jax.ShapeDtypeStruct((1, ff), F32),
            jax.ShapeDtypeStruct((1, d), F32),
            jax.ShapeDtypeStruct((1, d), F32),
        ],
        in_specs=[pl.BlockSpec(memory_space=V)] * 4,
        out_specs=[pl.BlockSpec(memory_space=V)] * 8,
    )(*parts)
    o_trunk, o_expand, o_shrink, o_in, o_hid, o_act, o_out, o_gain = out
    return (o_trunk, o_expand, o_shrink, o_in, o_hid, o_act, o_out, o_gain[0])


def solution(mesh):
    return jax.shard_map(
        functools.partial(body, mesh.shape["member"], mesh.shape["dp"]),
        mesh=mesh,
        in_specs=(
            P("dp", None),
            P(),
            P("member", None),
            P("member", None),
            P("member", None),
            P("member", None),
            P("member", None),
            P("member", None),
            P("member", "dp", None),
        ),
        out_specs=(
            P("dp", "member"),
            P("member", None),
            P("member", None),
            P("member", None),
            P("member", None),
            P("member", None),
            P("member", None),
            P(),
        ),
        check_vma=False,
    )
```

profile of v0, /device:TPU:0, one launch (start us, length us, event | category | flops | bytes accessed | tf_op | source)
XLA Modules:
  0.0 88.6 jit_solution(241048484443539768)
XLA Ops:
  0.6 85.3 %shard_map.152 = (bf16[394,128]{1,0:T(8,128)(2,1)}, bf16[4,8,32,256]{3,2,1,0:T(8,128)(2,1)}, bf16[4,64,1024]{2,1,0:T(8,128)(2,1)}, f32[1,7168]{1,0:T(1,128)}) custom-call(bf16[394,1024]{1,0:T(8,128)(2,1)} %trunk.1, f32[1,1024]{1,0:T(1,128)} %bitcast.4, bf16[128,2048]{1,0:T(8,128)(2,1)} %expand.1, bf16[256,1024]{1,0:T(8,128)(2,1)} %shrink.1, f32[1,1024]{1,0:T(1,128)} %r_in.1, ...), custom_call_target="tpu_custom_call" | custom-call | tf_op jit(solution)/shard_map/pallas_call | solution.py:434
  85.9 2.7 %shard_map.153 = (bf16[394,128]{1,0:T(8,128)(2,1)}, f32[128,2048]{1,0:T(8,128)}, f32[256,1024]{1,0:T(8,128)}, f32[1,1024]{1,0:T(1,128)}, f32[1,2048]{1,0:T(1,128...) custom-call(bf16[394,128]{1,0:T(8,128)(2,1)} %get-tuple-element.20.trunk, ...), custom_call_target="tpu_custom_call" | custom-call | tf_op jit(solution)/shard_map/pallas_call | solution.py:462
where the time goes:
time: 88.8 us; the launch traced here: 88.6 us
  Pallas kernels  87.9 us (99%)
    pallas_call x1, Pallas kernels, body(): pl.pallas_call(functools.partial(kernel, n, nz), out_shape=[jax.ShapeDtyp...  85.3 us
    pallas_call x1, Pallas kernels, body(): pl.pallas_call(functools.partial(finish, n, nz), out_shape=[jax.ShapeDtyp...  2.66 us

commit v1 on v0

--- a/solution.py
+++ b/solution.py
@@ -11,6 +11,9 @@
 coeff = 0.7978845608028654
 MESH = pl.DeviceIdType.MESH
 F32, BF16 = jnp.float32, jnp.bfloat16
+PARTS = (2, 2, 2, 2)
+RELAY_AT = 5
+VMEM_LIMIT = 64000 * 1024
 
 
 def gelu_pair(hidden):
@@ -478,9 +481,491 @@
     return (o_trunk, o_expand, o_shrink, o_in, o_hid, o_act, o_out, o_gain[0])
 
 
+def fast_kernel(names, cuts, *refs):
+    r = dict(zip(names, refs))
+    trunk, gain, expand, shrink, cot = (r[k] for k in ("trunk", "gain", "expand", "shrink", "cot"))
+    me = lax.axis_index("member")
+    mz = lax.axis_index("dp")
+    n, nz = 8, 4
+    tok, d = trunk.shape
+    ff = expand.shape[1]
+    fs, ds = ff // n, d // n
+    chunks = len(cuts)
+    offs = [sum(cuts[:c]) for c in range(chunks)]
+    top = tok // 32 * 16
+    rows = (pl.ds(0, top), pl.ds(top, tok - top))
+    core, xx, yy = me % 2, (me // 2) % 2, me // 4
+
+    def peer(s):
+        return (((yy + s // 4) % 2) * 2 + (xx + s // 2) % 2) * 2 + (core + s) % 2
+
+    def remote(src, dst, ss, rs, axis, who):
+        return pltpu.make_async_remote_copy(
+            src_ref=src, dst_ref=dst, send_sem=ss, recv_sem=rs,
+            device_id={axis: who}, device_id_type=MESH,
+        )
+
+    sc_send, sc_all, e_all, et = r["sc_send"], r["sc_all"], r["e_all"], r["et"]
+    for p in range(n):
+        sc_send[p, :, pl.ds(0, d)] = r["r_in"][...]
+        sc_send[p, :, pl.ds(d, d)] = r["r_out"][...]
+        sc_send[p, :, pl.ds(2 * d, fs)] = r["r_hid"][:, p * fs:(p + 1) * fs]
+        sc_send[p, :, pl.ds(2 * d + fs, fs)] = r["r_act"][:, p * fs:(p + 1) * fs]
+
+    barrier = pltpu.get_barrier_semaphore()
+    for s in range(1, n):
+        pl.semaphore_signal(barrier, inc=1, device_id={"member": peer(s)}, device_id_type=MESH)
+    for k in range(1, nz):
+        pl.semaphore_signal(barrier, inc=1, device_id={"dp": (mz + k) % nz}, device_id_type=MESH)
+    pl.semaphore_wait(barrier, n - 1 + nz - 1)
+
+    def e_cp(s):
+        p = peer(s)
+        return remote(
+            expand.at[:, pl.ds(pl.multiple_of(p * fs, fs), fs)], e_all.at[me],
+            r["sem_es"].at[s], r["sem_er"].at[me], "member", p)
+
+    def sc_cp(s):
+        p = peer(s)
+        return remote(sc_send.at[p], sc_all.at[me], r["sem_ss"].at[s], r["sem_sr"].at[me], "member", p)
+
+    def cots(c):
+        return r[f"cots{c}"]
+
+    def own_cp(c, s, h):
+        return remote(
+            cot.at[rows[h], pl.ds(offs[c], cuts[c])], cots(c).at[me, rows[h]],
+            r["sem_cs"].at[c, s, h], r["sem_cr"].at[c, me, h], "member", peer(s))
+
+    def fwd_cp(c, m, h, s, sem):
+        part = cots(c).at[m, rows[h]]
+        return remote(part, part, sem, r["sem_cr"].at[c, m, h], "member", peer(s))
+
+    def cross(c, h):
+        a, b = ((2, 4), (4, 2))[h]
+        return fwd_cp(c, peer(a), h, b, r["sem_fs"].at[c, h])
+
+    def near(c, s, h):
+        return fwd_cp(c, peer(s), h, 1, r["sem_ps"].at[c, s, h])
+
+    def cot_wait(c, m, h):
+        fwd_cp(c, m, h, 1, r["sem_fs"].at[c, 0]).wait_recv()
+
+    def own_far(c):
+        for h in range(2):
+            own_cp(c, 2, h).start()
+            own_cp(c, 4, 1 - h).start()
+
+    def relay(c):
+        cot_wait(c, peer(2), 0)
+        cross(c, 0).start()
+        cot_wait(c, peer(4), 1)
+        cross(c, 1).start()
+        if c + 2 < chunks:
+            own_far(c + 2)
+
+    order = [2, 4, 3, 5, 6, 7, 1]
+    for s in order:
+        sc_cp(s).start()
+    for s in order:
+        e_cp(s).start()
+    for c in range(chunks):
+        for h in range(2):
+            own_cp(c, 1, h).start()
+    for c in range(min(2, chunks)):
+        own_far(c)
+
+    e_all[me] = expand[:, pl.ds(pl.multiple_of(me * fs, fs), fs)]
+    sc_all[me] = sc_send[me]
+    for c in range(chunks):
+        cots(c)[me] = cot[:, offs[c]:offs[c] + cuts[c]]
+
+    normed_ref, inv_ref = r["normed"], r["inv"]
+    tokens = trunk[...].astype(F32)
+    centered = tokens - jnp.mean(tokens, axis=1, keepdims=True)
+    inv = lax.rsqrt(jnp.mean(centered * centered, axis=1, keepdims=True) + eps)
+    normed_ref[...] = centered * inv
+    inv_ref[...] = inv
+    s_acc, e_acc, b_acc, g_acc = r["s_acc"], r["e_acc"], r["b_acc"], r["g_acc"]
+    s_acc[...] = jnp.zeros_like(s_acc)
+    e_acc[...] = jnp.zeros_like(e_acc)
+    b_acc[...] = jnp.zeros_like(b_acc)
+    g_acc[...] = jnp.zeros_like(g_acc)
+
+    for s in order:
+        p = peer(s)
+        remote(sc_send.at[p], sc_all.at[p], r["sem_ss"].at[s], r["sem_sr"].at[p], "member", p).wait_recv()
+
+    si_all, sa_all = r["si_all"], r["sa_all"]
+    proj_all, act_all, slope_all, bact = r["proj_all"], r["act_all"], r["slope_all"], r["bact"]
+
+    @pl.loop(0, n)
+    def _(s):
+        s_in = sc_all[peer(s), :, pl.ds(0, d)]
+        si_all[s] = (normed_ref[...] * gain[...] * s_in).astype(BF16)
+
+    for s in order:
+        p = peer(s)
+        remote(e_all.at[p], e_all.at[p], r["sem_es"].at[s], r["sem_er"].at[p], "member", p).wait_recv()
+    et[...] = e_all[...].reshape(d, fs).T
+
+    @pl.loop(0, n)
+    def _(s):
+        @pl.when(s == RELAY_AT)
+        def _():
+            relay(0)
+
+        m = peer(s)
+        s_hid = sc_all[m, :, pl.ds(2 * d, fs)]
+        s_act = sc_all[m, :, pl.ds(2 * d + fs, fs)]
+        proj = dot(si_all[s], e_all[...].reshape(d, fs), 1, 0)
+        active, slope = gelu_pair(proj * s_hid)
+        proj_all[s] = proj
+        act_all[s] = active
+        slope_all[s] = slope * s_act
+        sa_all[s] = (active * s_act).astype(BF16)
+
+    inner = (mz == 1) | (mz == 2)
+    outer = (mz == 0) | (mz == 3)
+    pair = mz + 1 - 2 * (mz % 2)
+    across = 3 - mz
+
+    class Chain:
+        def __init__(self, refs, sem):
+            self.refs, self.sem = refs, sem
+
+        def hop(self, k):
+            own, in1, part, in2, fin = self.refs
+            src, dst, who = ((own, in1, pair), (part, in2, across), (fin, fin, pair))[k]
+            return remote(src, dst, self.sem(2 * k), self.sem(2 * k + 1), "dp", who)
+
+        def start(self):
+            @pl.when(outer)
+            def _():
+                self.hop(0).start()
+
+        def mid(self):
+            own, in1, part, in2, fin = self.refs
+
+            @pl.when(inner)
+            def _():
+                self.hop(0).wait_recv()
+                part[...] = (own[...].astype(F32) + in1[...].astype(F32)).astype(part.dtype)
+                self.hop(1).start()
+
+        def fin(self):
+            own, in1, part, in2, fin = self.refs
+
+            @pl.when(inner)
+            def _():
+                self.hop(1).wait_recv()
+                fin[...] = (part[...].astype(F32) + in2[...].astype(F32)).astype(fin.dtype)
+                self.hop(2).start()
+
+        def end(self):
+            @pl.when(outer)
+            def _():
+                self.hop(2).wait_recv()
+
+        def sent(self):
+            @pl.when(outer)
+            def _():
+                self.hop(0).wait_send()
+
+            @pl.when(inner)
+            def _():
+                self.hop(1).wait_send()
+                self.hop(2).wait_send()
+
+    red_s = [
+        Chain([r[f"s{k}_{c}"] for k in range(5)], lambda i, c=c: r["sem_zs"].at[i, c])
+        for c in range(chunks)
+    ]
+    red_e = [
+        Chain([r[f"e{k}"].at[peer(s)] for k in range(5)], lambda i, s=s: r["sem_ze"].at[i, s])
+        for s in range(n)
+    ]
+    red_t = Chain([r[f"t{k}"] for k in range(5)], lambda i: r["sem_zt"].at[i])
+
+    t_send, bp_all = r["t_send"], r["bp_all"]
+    for c in range(chunks):
+        cols = pl.ds(offs[c], cuts[c])
+        last = c == chunks - 1
+
+        @pl.loop(0, n)
+        def _(s):
+            m = peer(s)
+
+            @pl.when(s == 2)
+            def _():
+                cot_wait(c, peer(2), 1)
+                cot_wait(c, peer(4), 0)
+                for a in (2, 4):
+                    for h in range(2):
+                        near(c, a, h).start()
+
+            @pl.when(s == 6)
+            def _():
+                if not last:
+                    relay(c + 1)
+                if c >= 1:
+                    red_s[c - 1].mid()
+                if c >= 2:
+                    red_s[c - 2].fin()
+                for h in range(2):
+                    cot_wait(c, peer(6), h)
+                    near(c, 6, h).start()
+
+            @pl.when(s % 2 == 1)
+            def _():
+                cot_wait(c, m, 0)
+                cot_wait(c, m, 1)
+
+            s_out = sc_all[m, :, pl.ds(d + offs[c], cuts[c])]
+            scaled_cot = (cots(c)[m].astype(F32) * s_out).astype(BF16)
+            back_act = dot(scaled_cot, shrink[:, cols], 1, 1)
+            s_term = dot(sa_all[s], scaled_cot, 0, 0)
+            s_acc[:, cols] += s_term
+            t_send[m, :, pl.ds(d + offs[c], cuts[c])] = (
+                jnp.sum(s_term * shrink[:, cols].astype(F32), axis=0, keepdims=True) / s_out)
+            if c:
+                back_act = back_act + bact[s]
+            if not last:
+                bact[s] = back_act
+            else:
+                s_in = sc_all[m, :, pl.ds(0, d)]
+                s_hid = sc_all[m, :, pl.ds(2 * d, fs)]
+                g_act = jnp.sum(back_act * act_all[s], axis=0, keepdims=True)
+                back_hid = back_act * slope_all[s]
+                g_hid = jnp.sum(back_hid * proj_all[s], axis=0, keepdims=True)
+                back_proj = (back_hid * s_hid).astype(BF16)
+                bp_all[s] = back_proj
+                e_term = dot(back_proj, si_all[s], 0, 0)
+                e_acc[...] += e_term
+                e_sum = jnp.sum(e_term * et[...].astype(F32), axis=0, keepdims=True)
+                g_acc[...] += e_sum
+                t_send[m, :, pl.ds(0, d)] = e_sum / s_in
+                t_send[m, :, pl.ds(3 * d, fs)] = g_hid
+                t_send[m, :, pl.ds(3 * d + fs, fs)] = g_act
+
+        r[f"s0_{c}"][...] = s_acc[:, cols].astype(BF16)
+        red_s[c].start()
+
+    e_send, e_recv, t_recv = r["e_send"], r["e0"], r["t_recv"]
+    u_send, u_recv = r["u_send"], r["u_recv"]
+
+    def ge_cp(s):
+        p = peer(s)
+        return remote(e_send.at[p], e_recv.at[me], r["sem_gs"].at[s], r["sem_gr"].at[me], "member", p)
+
+    def ge_wait(s):
+        p = peer(s)
+        remote(e_send.at[p], e_recv.at[p], r["sem_gs"].at[s], r["sem_gr"].at[p], "member", p).wait_recv()
+
+    def t_cp(s):
+        p = peer(s)
+        return remote(t_send.at[p], t_recv.at[me], r["sem_ts"].at[s], r["sem_tr"].at[me], "member", p)
+
+    def u_cp(s):
+        p = peer(s)
+        return remote(u_send.at[p], u_recv.at[me], r["sem_us"].at[s], r["sem_ur"].at[me], "member", p)
+
+    e_send[...] = e_acc[...].astype(BF16).T.reshape(n, ds, fs)
+    tail = [1, 2, 4, 3, 5, 6, 7]
+    for s in tail:
+        ge_cp(s).start()
+    e_recv[me] = e_send[me]
+    red_e[0].start()
+
+    g_part = g_acc[...] / gain[...]
+    for p in range(n):
+        t_send[p, :, pl.ds(2 * d, d)] = g_part
+    for s in tail:
+        t_cp(s).start()
+    t_recv[me] = t_send[me]
+
+    def back_loop(lo, hi):
+        @pl.loop(lo, hi)
+        def _(s):
+            s_in = sc_all[peer(s), :, pl.ds(0, d)]
+            b_acc[...] += dot(bp_all[s], et[...], 1, 0) * s_in
+
+    back_loop(0, n // 2)
+    ge_wait(1)
+    red_e[1].start()
+    back_loop(n // 2, n)
+
+    unit = b_acc[...] * gain[...]
+    normed = normed_ref[...]
+    term = cot[...].astype(F32) + inv_ref[...] * (
+        unit
+        - jnp.mean(unit, axis=1, keepdims=True)
+        - normed * jnp.mean(unit * normed, axis=1, keepdims=True)
+    )
+    term = term.astype(BF16)
+    for p in range(n):
+        u_send[p] = term[:, p * ds:(p + 1) * ds]
+    for s in tail:
+        u_cp(s).start()
+
+    if chunks > 1:
+        red_s[chunks - 2].fin()
+    red_s[chunks - 1].mid()
+    red_e[0].mid()
+    for s in (2, 4):
+        ge_wait(s)
+        red_e[s].start()
+    red_e[1].mid()
+    for s in tail:
+        p = peer(s)
+        remote(t_send.at[p], t_recv.at[p], r["sem_ts"].at[s], r["sem_tr"].at[p], "member", p).wait_recv()
+    t_sum = r["t0"]
+    t_sum[:, pl.ds(0, 3 * d)] = sum(t_recv[p, :, pl.ds(0, 3 * d)] for p in range(n))
+    for p in range(n):
+        t_sum[:, pl.ds(3 * d + p * fs, fs)] = t_recv[p, :, pl.ds(3 * d, fs)]
+        t_sum[:, pl.ds(3 * d + ff + p * fs, fs)] = t_recv[p, :, pl.ds(3 * d + fs, fs)]
+    red_t.start()
+    for s in (3, 5):
+        ge_wait(s)
+        red_e[s].start()
+    red_s[chunks - 1].fin()
+    red_e[0].fin()
+    red_e[2].mid()
+    red_e[1].fin()
+    red_e[4].mid()
+    for s in (6, 7):
+        ge_wait(s)
+        red_e[s].start()
+    red_e[2].fin()
+    red_t.mid()
+    red_e[3].mid()
+    red_e[4].fin()
+    red_e[5].mid()
+    red_t.fin()
+    red_e[3].fin()
+    red_e[6].mid()
+    red_e[5].fin()
+    red_e[7].mid()
+
+    total = u_send[me].astype(F32)
+    for s in tail:
+        p = peer(s)
+        remote(u_send.at[p], u_recv.at[p], r["sem_us"].at[s], r["sem_ur"].at[p], "member", p).wait_recv()
+        total += u_recv[p].astype(F32)
+    r["o_trunk"][...] = total.astype(BF16)
+
+    red_e[6].fin()
+    red_e[7].fin()
+    for c in range(chunks):
+        red_s[c].end()
+        r["o_shrink"][:, pl.ds(offs[c], cuts[c])] = r[f"s4_{c}"][...]
+    red_t.end()
+    r["o_small"][...] = r["t4"][...]
+    for s in (0, 1, 2, 4, 3, 5, 6, 7):
+        red_e[s].end()
+        r["o_expand"][peer(s)] = r["e4"][peer(s)]
+
+    for chain in (*red_s, *red_e, red_t):
+        chain.sent()
+    for s in order:
+        for copy in (sc_cp, e_cp, ge_cp, t_cp, u_cp):
+            copy(s).wait_send()
+    for c in range(chunks):
+        for h in range(2):
+            for s in (1, 2, 4):
+                own_cp(c, s, h).wait_send()
+            cross(c, h).wait_send()
+            for s in (2, 4, 6):
+                near(c, s, h).wait_send()
+
+
+def fast_finish(n, trunk, expand, shrink, small, o_trunk, o_expand, o_shrink, o_in, o_hid, o_act, o_out, o_gain):
+    d, ff = o_in.shape[1], o_hid.shape[1]
+    fs = expand.shape[2]
+    o_trunk[...] = trunk[...]
+    o_in[...] = small[:, pl.ds(0, d)]
+    o_out[...] = small[:, pl.ds(d, d)]
+    o_gain[...] = small[:, pl.ds(2 * d, d)]
+    o_hid[...] = small[:, pl.ds(3 * d, ff)]
+    o_act[...] = small[:, pl.ds(3 * d + ff, ff)]
+    o_shrink[...] = shrink[...].astype(F32)
+    for p in range(n):
+        o_expand[:, pl.ds(p * fs, fs)] = expand[p].astype(F32)
+
+
+def fast_body(trunk, normgain, expand, shrink, inscale, hidscale, actscale, outscale, cotangent):
+    n = 8
+    tok, d = trunk.shape
+    ff = expand.shape[1]
+    fs, ds = ff // n, d // n
+    cuts = [d * part // sum(PARTS) for part in PARTS]
+    chunks = len(cuts)
+    V = pltpu.VMEM
+    DMA = pltpu.SemaphoreType.DMA
+    width, small, small2 = 2 * d + 2 * fs, 3 * d + 2 * fs, 3 * d + 2 * ff
+    args = ["trunk", "gain", "expand", "shrink", "r_in", "r_out", "r_hid", "r_act", "cot"]
+    outs = ["o_trunk", "o_expand", "o_shrink", "o_small"]
+    scratch = dict(
+        sc_send=V((n, 1, width), F32), sc_all=V((n, 1, width), F32),
+        e_all=V((n, ds, fs), BF16), et=V((fs, d), BF16),
+        si_all=V((n, tok, d), BF16), sa_all=V((n, tok, fs), BF16), bp_all=V((n, tok, fs), BF16),
+        proj_all=V((n, tok, fs), F32), act_all=V((n, tok, fs), F32), slope_all=V((n, tok, fs), F32),
+        bact=V((n, tok, fs), F32),
+        normed=V((tok, d), F32), inv=V((tok, 1), F32),
+        b_acc=V((tok, d), F32), s_acc=V((fs, d), F32), e_acc=V((fs, d), F32), g_acc=V((1, d), F32),
+        e_send=V((n, ds, fs), BF16),
+        t_send=V((n, 1, small), F32), t_recv=V((n, 1, small), F32),
+        u_send=V((n, tok, ds), BF16), u_recv=V((n, tok, ds), BF16),
+        sem_es=DMA((n,)), sem_er=DMA((n,)), sem_ss=DMA((n,)), sem_sr=DMA((n,)),
+        sem_cs=DMA((chunks, n, 2)), sem_cr=DMA((chunks, n, 2)), sem_fs=DMA((chunks, 2)), sem_ps=DMA((chunks, n, 2)),
+        sem_gs=DMA((n,)), sem_gr=DMA((n,)), sem_ts=DMA((n,)), sem_tr=DMA((n,)), sem_us=DMA((n,)), sem_ur=DMA((n,)),
+        sem_zs=DMA((6, chunks)), sem_ze=DMA((6, n)), sem_zt=DMA((6,)),
+    )
+    for c in range(chunks):
+        scratch[f"cots{c}"] = V((n, tok, cuts[c]), BF16)
+    for k in range(5):
+        scratch[f"e{k}"] = V((n, ds, fs), BF16)
+        scratch[f"t{k}"] = V((1, small2), F32)
+        for c in range(chunks):
+            scratch[f"s{k}_{c}"] = V((fs, cuts[c]), BF16)
+    parts = pl.pallas_call(
+        functools.partial(fast_kernel, [*args, *outs, *scratch], cuts),
+        out_shape=[
+            jax.ShapeDtypeStruct((tok, ds), BF16),
+            jax.ShapeDtypeStruct((n, ds, fs), BF16),
+            jax.ShapeDtypeStruct((fs, d), BF16),
+            jax.ShapeDtypeStruct((1, small2), F32),
+        ],
+        in_specs=[pl.BlockSpec(memory_space=V)] * 9,
+        out_specs=[pl.BlockSpec(memory_space=V)] * 4,
+        scratch_shapes=list(scratch.values()),
+        compiler_params=pltpu.CompilerParams(
+            collective_id=0, has_side_effects=True, vmem_limit_bytes=VMEM_LIMIT
+        ),
+    )(trunk, normgain[None], expand, shrink, inscale, outscale, hidscale, actscale, cotangent[0])
+    out = pl.pallas_call(
+        functools.partial(fast_finish, n),
+        out_shape=[
+            jax.ShapeDtypeStruct((tok, ds), BF16),
+            jax.ShapeDtypeStruct((ds, ff), F32),
+            jax.ShapeDtypeStruct((fs, d), F32),
+            jax.ShapeDtypeStruct((1, d), F32),
+            jax.ShapeDtypeStruct((1, ff), F32),
+            jax.ShapeDtypeStruct((1, ff), F32),
+            jax.ShapeDtypeStruct((1, d), F32),
+            jax.ShapeDtypeStruct((1, d), F32),
+        ],
+        in_specs=[pl.BlockSpec(memory_space=V)] * 4,
+        out_specs=[pl.BlockSpec(memory_space=V)] * 8,
+    )(*parts)
+    o_trunk, o_expand, o_shrink, o_in, o_hid, o_act, o_out, o_gain = out
+    return (o_trunk, o_expand, o_shrink, o_in, o_hid, o_act, o_out, o_gain[0])
+
+
 def solution(mesh):
+    n, nz = mesh.shape["member"], mesh.shape["dp"]
     return jax.shard_map(
-        functools.partial(body, mesh.shape["member"], mesh.shape["dp"]),
+        fast_body if (n, nz) == (8, 4) else functools.partial(body, n, nz),
         mesh=mesh,
         in_specs=(
             P("dp", None),

time: 88.8 us -> 83.9 us (0.945)
  Pallas kernels: 87.9 us -> 83 us
    pallas_call x2, Pallas kernels: 87.9 us -> 83 us  [the longest x1 80.4 us: fast_body(): pl.pallas_call(functools.partial(fast_kernel, [*args, *outs, *scratch], c...]
where the time goes in v1:
time: 83.9 us; the launch traced here: 83.7 us
  Pallas kernels  83 us (99%)
    pallas_call x1, Pallas kernels, fast_body(): pl.pallas_call(functools.partial(fast_kernel, [*args, *outs, *scratch], c...  80.4 us
    pallas_call x1, Pallas kernels, fast_body(): pl.pallas_call(functools.partial(fast_finish, n), out_shape=[jax.ShapeDty...  2.66 us

profile of v1, /device:TPU:0, one launch (start us, length us, event | category | flops | bytes accessed | tf_op | source)
XLA Modules:
  0.0 83.7 jit_solution(10555396630125453929)
XLA Ops:
  0.6 80.4 %shard_map.152 = (bf16[394,128]{1,0:T(8,128)(2,1)}, bf16[8,128,256]{2,1,0:T(8,128)(2,1)}, bf16[256,1024]{1,0:T(8,128)(2,1)}, f32[1,7168]{1,0:T(1,128)}) custom-call(bf16[394,1024]{1,0:T(8,128)(2,1)} %refs_0_.1, f32[1,1024]{1,0:T(1,128)} %bitcast.4, bf16[128,2048]{1,0:T(8,128)(2,1)} %refs_2_.1, bf16[256,1024]{1,0:T(8,128)(2,1)} %refs_3_.1, ...), custom_call_target="tpu_custom_call" | custom-call | tf_op jit(solution)/shard_map/pallas_call | solution.py:931
  81.0 2.7 %shard_map.153 = (bf16[394,128]{1,0:T(8,128)(2,1)}, f32[128,2048]{1,0:T(8,128)}, f32[256,1024]{1,0:T(8,128)}, f32[1,1024]{1,0:T(1,128)}, f32[1,2048]{1,0:T(1,128...) custom-call(bf16[394,128]{1,0:T(8,128)(2,1)} %get-tuple-element.20.trunk, ...), custom_call_target="tpu_custom_call" | custom-call | tf_op jit(solution)/shard_map/pallas_call | solution.py:946
